TPU v7x, 256 devices: a whole 4x4x8 slice. The times are simulated.
256 devices in a mesh: dp: 8 (over x, core), fsdp: 8 (over z), mp: 4 (over y).
Axes of the slice: x: 4, y: 4, z: 8, core: 2. Of those that a mesh axis runs over, the one named last changes fastest.
Arguments:
- gradients: bfloat16 [64, 12, 2, 256, 1024], P(('dp', 'fsdp'), None, None, None, 'mp'), may hold values from -16 to 16
- master: float32 [12, 2, 256, 1024], P(None, None, ('dp', 'fsdp'), 'mp'), may hold values from -0.375 to 0.375
- teacher: float32 [12, 2, 256, 1024], P(None, None, ('dp', 'fsdp'), 'mp'), may hold values from -0.375 to 0.375
- first_moment: float32 [12, 2, 256, 1024], P(None, None, ('dp', 'fsdp'), 'mp'), may hold values from -2.2888184e-05 to 2.2888184e-05
- second_moment: float32 [12, 2, 256, 1024], P(None, None, ('dp', 'fsdp'), 'mp'), may hold values from 0 to 1, as said below
- layer_rates: float32 [12], replicated, may hold values from 0.02 to 0.2
Outputs:
- master_new: float32 [12, 2, 256, 1024], P(None, None, ('dp', 'fsdp'), 'mp')
- teacher_new: float32 [12, 2, 256, 1024], P(None, None, ('dp', 'fsdp'), 'mp')
- first_new: float32 [12, 2, 256, 1024], P(None, None, ('dp', 'fsdp'), 'mp')
- second_new: float32 [12, 2, 256, 1024], P(None, None, ('dp', 'fsdp'), 'mp')
- student_weights: bfloat16 [12, 2, 256, 1024], P(None, None, None, 'mp')
- teacher_weights: bfloat16 [12, 2, 256, 1024], P(None, None, None, 'mp')
Inputs may be any that keep to these rules, and one draw needn't show every extreme that they name: `second_moment`: every entry is positive.
All inputs are finite; a program needn't handle non-finite values.
Results may differ from a plain program's by a relative error of at most 0.0004.
Values may be sent and summed in bfloat16 or wider, within the bound.
No kernel may reach another device: no remote copies, remote signals or barrier semaphores. Data moves between devices by JAX's collectives and lax.ppermute only.
A program may use at most 64 MiB of HBM per device.

v0:
```python
import jax
import jax.numpy as jnp
from jax import lax
from jax.sharding import PartitionSpec as P

OWN = ("dp", "fsdp")
ALL = ("dp", "fsdp", "mp")
CLIP_NORM = 0.1
BETA_ONE = 0.9
BETA_TWO = 0.999
BIAS_ONE = 1.0 - 0.9**50 * 0.9**50
BIAS_TWO = 1.0 - 0.999**50 * 0.999**50
ADAM_EPS = 1e-08
DECAY = 0.05
EMA_KEEP = 0.95


def shards(gradients, master, teacher, first_moment, second_moment, layer_rates):
    own_grad = gradients[0].astype(jnp.float32)
    summed = lax.psum_scatter(own_grad, OWN, scatter_dimension=2, tiled=True)
    mean_grad = summed / 64.0
    norm_sq = lax.psum(jnp.sum(mean_grad * mean_grad), ALL)
    clip_factor = jnp.minimum(1.0, CLIP_NORM / (jnp.sqrt(norm_sq) + 1e-06))
    clipped = clip_factor * mean_grad
    first_new = BETA_ONE * first_moment + (1.0 - BETA_ONE) * clipped
    second_new = BETA_TWO * second_moment + (1.0 - BETA_TWO) * clipped * clipped
    direction = first_new / BIAS_ONE / (jnp.sqrt(second_new / BIAS_TWO) + ADAM_EPS) + DECAY * master
    layer_rate = layer_rates[:, None, None, None]
    master_new = master - layer_rate * direction
    teacher_new = EMA_KEEP * teacher + (1.0 - EMA_KEEP) * master_new
    student = lax.all_gather(master_new.astype(jnp.bfloat16), OWN, axis=2, tiled=True)
    teach = lax.all_gather(teacher_new.astype(jnp.bfloat16), OWN, axis=2, tiled=True)
    return (master_new, teacher_new, first_new, second_new, student, teach)


def solution(mesh):
    own = P(None, None, OWN, "mp")
    gathered = P(None, None, None, "mp")
    in_specs = (P(OWN, None, None, None, "mp"), own, own, own, own, P())
    out_specs = (own, own, own, own, gathered, gathered)
    return jax.shard_map(shards, mesh=mesh, in_specs=in_specs, out_specs=out_specs, check_vma=False)
```

profile of v0, /device:TPU:1, one launch (start us, length us, event | category | flops | bytes accessed | tf_op | source)
XLA Modules:
  0.0 413.0 jit_solution(480780248336302537)
XLA Ops:
  7.2 0.0 reduce-scatter.2.cloned.1.call-start
  7.2 7.0 %bitcast_convert_fusion = f32[12,2,256,256]{3,0,1,2:T(8,128)} fusion(bf16[1,12,2,256,256]{4,3,2,1,0:T(8,128)(2,1)} %param.6), kind=kLoop, calls=%fused_computation | loop fusion | flops 1572864 | bytes 9437184 | tf_op jit(solution)/shard_map/convert_element_type | solution.py:19
  14.2 0.0 copy-start
  14.2 0.0 copy-start.1
  14.2 0.0 copy-start.2
  14.2 0.0 copy-start.3
  14.2 0.0 copy-start.4
  14.2 0.0 reduce-scatter.2.cloned.1.call-update
  14.3 0.0 all-gather.3.cloned.1.call-start
  14.3 151.8 %reduce-scatter.2.cloned.1.call-done = f32[12,2,4,256]{3,0,1,2:T(8,128)} async-done(((f32[12,2,256,256]{3,0,1,2:T(8,128)}), f32[12,2,4,256]{3,0,1,2:T(8,128)}) %reduce-scatter.2.cloned.1.call-update) | async-done | bytes 98320 | tf_op jit(solution)/shard_map/reduce_scatter | solution.py:20
  166.1 1.5 multiply_reduce_fusion
  167.6 78.7 %psum.7 = f32[]{:T(128)} all-reduce(f32[]{:T(128)} %multiply_reduce_fusion), channel_id=1, replica_groups=mesh['dp'=8,'fsdp'=8,'mp'=4] {'dp','fsdp','mp'}, use_global_device_ids=true, to_apply=%region_2.0 | all-reduce | flops 1 | bytes 8 | tf_op jit(solution)/shard_map/psum | solution.py:22
  247.1 0.0 copy-done
  247.1 0.0 copy-done.1
  247.1 0.0 copy-done.2
  247.1 0.0 copy-done.3
  247.1 0.0 copy-done.4
  247.1 1.1 fusion.5
  248.3 0.7 copy.18
  248.9 0.0 all-gather.3.cloned.1.call-update
  249.0 0.0 all-gather.5.cloned.1.call-start
  249.0 0.7 copy.19
  249.7 0.0 all-gather.5.cloned.1.call-update
  249.7 0.7 copy.20
  250.4 0.7 copy.21
  251.1 0.7 copy.22
  251.8 0.7 copy.23
  252.5 71.5 %all-gather.3.cloned.1.call-done = bf16[12,2,256,256]{3,1,0,2:T(2,128)(2,1)} async-done(((bf16[12,2,4,256]{3,1,0,2:T(2,128)(2,1)}), bf16[12,2,256,256]{3,1,0,2:T(2,128)(2,1)}) %all-gather.3.cloned.1.call-update) | async-done | bytes 3145744 | tf_op jit(solution)/shard_map/all_gather | solution.py:31
  324.1 4.3 %copy.24 = bf16[12,2,256,256]{3,2,1,0:T(8,128)(2,1)} copy(bf16[12,2,256,256]{3,1,0,2:T(2,128)(2,1)} %all-gather.3.cloned.1.call-done) | data formatting | bytes 6291456
  328.4 73.9 %all-gather.5.cloned.1.call-done = bf16[12,2,256,256]{3,1,0,2:T(2,128)(2,1)} async-done(((bf16[12,2,4,256]{3,1,0,2:T(2,128)(2,1)}), bf16[12,2,256,256]{3,1,0,2:T(2,128)(2,1)}) %all-gather.5.cloned.1.call-update) | async-done | bytes 3145744 | tf_op jit(solution)/shard_map/all_gather | solution.py:32
  402.2 4.3 %copy.25 = bf16[12,2,256,256]{3,2,1,0:T(8,128)(2,1)} copy(bf16[12,2,256,256]{3,1,0,2:T(2,128)(2,1)} %all-gather.5.cloned.1.call-done) | data formatting | bytes 6291456
  (1 shorter events, 0.0 us)
Async XLA Ops:
  7.2 158.9 %reduce-scatter.2.cloned.1.call-start = ((), (), s32[]{:S(2)}) async-start(), calls=%async_computation.1 | async-start | bytes 8519680 | tf_op jit(solution)/shard_map/reduce_scatter | solution.py:20
  14.2 232.9 %copy-start = (f32[12,2,4,256]{3,2,1,0:T(4,128)S(1)}, f32[12,2,4,256]{3,2,1,0:T(4,128)}, u32[]{:S(2)}) copy-start(f32[12,2,4,256]{3,2,1,0:T(4,128)} %param.8) | copy-start | bytes 294916
  14.2 232.9 %copy-start.1 = (f32[12,2,4,256]{3,2,1,0:T(4,128)S(1)}, f32[12,2,4,256]{3,2,1,0:T(4,128)}, u32[]{:S(2)}) copy-start(f32[12,2,4,256]{3,2,1,0:T(4,128)} %param.7) | copy-start | bytes 294916
  14.2 232.9 %copy-start.2 = (f32[12,2,4,256]{3,2,1,0:T(4,128)S(1)}, f32[12,2,4,256]{3,2,1,0:T(4,128)}, u32[]{:S(2)}) copy-start(f32[12,2,4,256]{3,2,1,0:T(4,128)} %param.9) | copy-start | bytes 294916
  14.2 232.9 %copy-start.3 = (f32[12,2,4,256]{3,2,1,0:T(4,128)S(1)}, f32[12,2,4,256]{3,2,1,0:T(4,128)}, u32[]{:S(2)}) copy-start(f32[12,2,4,256]{3,2,1,0:T(4,128)} %param.10) | copy-start | bytes 294916
  14.2 232.9 %copy-start.4 = (f32[12]{0:T(128)S(1)}, f32[12]{0:T(128)}, u32[]{:S(2)}) copy-start(f32[12]{0:T(128)} %param.11) | copy-start | bytes 148
  14.3 309.8 %all-gather.3.cloned.1.call-start = ((), (), s32[]{:S(2)}) async-start(), calls=%async_computation.2 | async-start | bytes 3194880 | tf_op jit(solution)/shard_map/all_gather | solution.py:31
  249.0 153.3 %all-gather.5.cloned.1.call-start = ((), (), s32[]{:S(2)}) async-start(), calls=%async_computation.3 | async-start | bytes 3194880 | tf_op jit(solution)/shard_map/all_gather | solution.py:32
Sparse Core Ops, SparseCore 0:
  14.4 151.6 reduce-scatter.1
  249.1 74.9 all-gather.2
  326.8 75.3 all-gather.4
where the time goes:
time: 413 us
  waiting for transfers between devices  297 us (72%)
  blocking collectives  78.7 us (19%)
  between operations  14.5 us (4%)
  local copies, waits for them, and re-layouts  12.7 us (3%)
  other arithmetic  9.68 us (2%)
    reduce_scatter x1, waiting for transfers between devices, shards(): summed = lax.psum_scatter(own_grad, OWN, scatter_dimension=2, tiled=True)  152 us
    psum x1, blocking collectives, shards(): norm_sq = lax.psum(jnp.sum(mean_grad * mean_grad), ALL)  78.7 us
    all_gather x1, waiting for transfers between devices, shards(): lax.all_gather(teacher_new.astype(jnp.bfloat16), OWN, axis=2, tiled=True)  73.9 us
    all_gather x1, waiting for transfers between devices, shards(): lax.all_gather(master_new.astype(jnp.bfloat16), OWN, axis=2, tiled=True)  71.5 us
    unnamed x16, local copies, waits for them, and re-layouts  11.4 us
  transfers between devices with their start and end apart: 3, of which 3 were waited for; matrix products, arithmetic and copies ran while one was open for 2% of the time, Pallas kernels for 0%

commit v1 on v0

--- a/solution.py
+++ b/solution.py
@@ -15,6 +15,12 @@
 EMA_KEEP = 0.95
 
 
+def _switch_state(mine, lane_axis):
+    local_next = lax.all_gather(mine, lane_axis)
+    big = jnp.concatenate(local_next, 2)
+    return big
+
+
 def shards(gradients, master, teacher, first_moment, second_moment, layer_rates):
     own_grad = gradients[0].astype(jnp.float32)
     summed = lax.psum_scatter(own_grad, OWN, scatter_dimension=2, tiled=True)
@@ -28,7 +34,7 @@
     layer_rate = layer_rates[:, None, None, None]
     master_new = master - layer_rate * direction
     teacher_new = EMA_KEEP * teacher + (1.0 - EMA_KEEP) * master_new
-    student = lax.all_gather(master_new.astype(jnp.bfloat16), OWN, axis=2, tiled=True)
+    student = _switch_state(master_new.astype(jnp.bfloat16), OWN)
     teach = lax.all_gather(teacher_new.astype(jnp.bfloat16), OWN, axis=2, tiled=True)
     return (master_new, teacher_new, first_new, second_new, student, teach)
 

time: 413 us -> 413 us (level)
    reshape x0 -> x2, local copies, waits for them, and re-layouts: none -> 6.44 us  [_switch_state(): big = jnp.concatenate(local_next, 2)]
    unnamed x16 -> x15, local copies, waits for them, and re-layouts: 11.4 us -> 7.13 us
where the time goes in v1:
time: 413 us
  waiting for transfers between devices  295 us (71%)
  blocking collectives  78.7 us (19%)
  local copies, waits for them, and re-layouts  14.9 us (4%)
  between operations  14.6 us (4%)
  other arithmetic  9.68 us (2%)
    reduce_scatter x1, waiting for transfers between devices, shards(): summed = lax.psum_scatter(own_grad, OWN, scatter_dimension=2, tiled=True)  152 us
    psum x1, blocking collectives, shards(): norm_sq = lax.psum(jnp.sum(mean_grad * mean_grad), ALL)  78.7 us
    all_gather x1, waiting for transfers between devices, shards(): lax.all_gather(teacher_new.astype(jnp.bfloat16), OWN, axis=2, tiled=True)  71.7 us
    all_gather x1, waiting for transfers between devices, _switch_state(): local_next = lax.all_gather(mine, lane_axis)  71.5 us
  transfers between devices with their start and end apart: 3, of which 3 were waited for; matrix products, arithmetic and copies ran while one was open for 2% of the time, Pallas kernels for 0%

profile of v1, /device:TPU:1, one launch (start us, length us, event | category | flops | bytes accessed | tf_op | source)
XLA Modules:
  0.0 413.0 jit_solution(5299644475290063555)
XLA Ops:
  7.2 0.0 reduce-scatter.2.cloned.1.call-start
  7.2 7.0 %bitcast_convert_fusion = f32[12,2,256,256]{3,0,1,2:T(8,128)} fusion(bf16[1,12,2,256,256]{4,3,2,1,0:T(8,128)(2,1)} %param.6), kind=kLoop, calls=%fused_computation | loop fusion | flops 1572864 | bytes 9437184 | tf_op jit(solution)/shard_map/convert_element_type | solution.py:25
  14.2 0.0 copy-start
  14.2 0.0 copy-start.1
  14.2 0.0 copy-start.2
  14.2 0.0 copy-start.3
  14.2 0.0 copy-start.4
  14.2 0.0 reduce-scatter.2.cloned.1.call-update
  14.3 0.0 all-gather.6.cloned.1.call-start
  14.3 151.8 %reduce-scatter.2.cloned.1.call-done = f32[12,2,4,256]{3,0,1,2:T(8,128)} async-done(((f32[12,2,256,256]{3,0,1,2:T(8,128)}), f32[12,2,4,256]{3,0,1,2:T(8,128)}) %reduce-scatter.2.cloned.1.call-update) | async-done | bytes 98320 | tf_op jit(solution)/shard_map/reduce_scatter | solution.py:26
  166.1 1.5 multiply_reduce_fusion
  167.6 78.7 %psum.7 = f32[]{:T(128)} all-reduce(f32[]{:T(128)} %multiply_reduce_fusion), channel_id=1, replica_groups=mesh['dp'=8,'fsdp'=8,'mp'=4] {'dp','fsdp','mp'}, use_global_device_ids=true, to_apply=%region_2.0 | all-reduce | flops 1 | bytes 8 | tf_op jit(solution)/shard_map/psum | solution.py:28
  247.1 0.0 copy-done
  247.1 0.0 copy-done.1
  247.1 0.0 copy-done.2
  247.1 0.0 copy-done.3
  247.1 0.0 copy-done.4
  247.1 1.1 fusion.5
  248.3 0.7 copy.19
  248.9 0.0 all-gather.6.cloned.1.call-update
  249.0 0.0 all-gather.4.cloned.1.call-start
  249.0 0.7 copy.21
  249.7 0.0 all-gather.4.cloned.1.call-update
  249.7 0.7 copy.22
  250.4 0.7 copy.23
  251.1 0.7 copy.24
  251.8 0.7 copy.25
  252.5 71.5 %all-gather.6.cloned.1.call-done = bf16[768,2,4,256]{3,2,1,0:T(4,128)(2,1)} async-done(((bf16[12,2,4,256]{3,2,1,0:T(4,128)(2,1)}), bf16[768,2,4,256]{3,2,1,0:T(4,128)(2,1)}) %all-gather.6.cloned.1.call-update) | async-done | bytes 3145744 | tf_op jit(solution)/shard_map/all_gather | solution.py:19
  324.1 3.5 copy.20
  327.6 2.9 reshape.22
  330.5 71.7 %all-gather.4.cloned.1.call-done = bf16[12,2,256,256]{3,1,0,2:T(2,128)(2,1)} async-done(((bf16[12,2,4,256]{3,1,0,2:T(2,128)(2,1)}), bf16[12,2,256,256]{3,1,0,2:T(2,128)(2,1)}) %all-gather.4.cloned.1.call-update) | async-done | bytes 3145744 | tf_op jit(solution)/shard_map/all_gather | solution.py:38
  402.2 4.3 %copy.26 = bf16[12,2,256,256]{3,2,1,0:T(8,128)(2,1)} copy(bf16[12,2,256,256]{3,1,0,2:T(2,128)(2,1)} %all-gather.4.cloned.1.call-done) | data formatting | bytes 6291456
  (1 shorter events, 0.0 us)
Async XLA Ops:
  7.2 158.9 %reduce-scatter.2.cloned.1.call-start = ((), (), s32[]{:S(2)}) async-start(), calls=%async_computation.1 | async-start | bytes 8519680 | tf_op jit(solution)/shard_map/reduce_scatter | solution.py:26
  14.2 232.9 %copy-start = (f32[12,2,4,256]{3,2,1,0:T(4,128)S(1)}, f32[12,2,4,256]{3,2,1,0:T(4,128)}, u32[]{:S(2)}) copy-start(f32[12,2,4,256]{3,2,1,0:T(4,128)} %param.8) | copy-start | bytes 294916
  14.2 232.9 %copy-start.1 = (f32[12,2,4,256]{3,2,1,0:T(4,128)S(1)}, f32[12,2,4,256]{3,2,1,0:T(4,128)}, u32[]{:S(2)}) copy-start(f32[12,2,4,256]{3,2,1,0:T(4,128)} %param.7) | copy-start | bytes 294916
  14.2 232.9 %copy-start.2 = (f32[12,2,4,256]{3,2,1,0:T(4,128)S(1)}, f32[12,2,4,256]{3,2,1,0:T(4,128)}, u32[]{:S(2)}) copy-start(f32[12,2,4,256]{3,2,1,0:T(4,128)} %param.9) | copy-start | bytes 294916
  14.2 232.9 %copy-start.3 = (f32[12,2,4,256]{3,2,1,0:T(4,128)S(1)}, f32[12,2,4,256]{3,2,1,0:T(4,128)}, u32[]{:S(2)}) copy-start(f32[12,2,4,256]{3,2,1,0:T(4,128)} %param.10) | copy-start | bytes 294916
  14.2 232.9 %copy-start.4 = (f32[12]{0:T(128)S(1)}, f32[12]{0:T(128)}, u32[]{:S(2)}) copy-start(f32[12]{0:T(128)} %param.11) | copy-start | bytes 148
  14.3 309.8 %all-gather.6.cloned.1.call-start = ((), (), s32[]{:S(2)}) async-start(), calls=%async_computation.3 | async-start | bytes 3194880 | tf_op jit(solution)/shard_map/all_gather | solution.py:19
  249.0 153.3 %all-gather.4.cloned.1.call-start = ((), (), s32[]{:S(2)}) async-start(), calls=%async_computation.2 | async-start | bytes 3194880 | tf_op jit(solution)/shard_map/all_gather | solution.py:38
Sparse Core Ops, SparseCore 0:
  14.4 151.6 reduce-scatter.1
  249.1 74.9 all-gather.5
  326.8 75.3 all-gather.3
